TPU v7x, 8 devices: a whole 2x2x1 slice. The times are simulated.
8 devices in a mesh: dp: 2 (over z, y), sp: 4 (over x, core).
Axes of the slice: x: 2, y: 2, z: 1, core: 2. Of those that a mesh axis runs over, the one named last changes fastest.
Arguments:
- x_in: bfloat16 [8, 4096, 2560], P('dp', 'sp'), parts along dimension 0
- dy_in: bfloat16 [8, 4096, 2560], P('dp', 'sp'), parts along dimension 0
- positions: int32 [8192], P(('dp', 'sp')), parts along dimension 0
- w_q: bfloat16 [2560, 2048], replicated
- w_k: bfloat16 [2560, 1024], replicated
- w_v: bfloat16 [2560, 1024], replicated
- w_o: bfloat16 [2048, 2560], replicated
- w_pre: float32 [2560], replicated
- w_post: float32 [2560], replicated
- q_norm: float32 [256], replicated
- k_norm: float32 [256], replicated
Outputs:
- output 1: bfloat16 [8, 4096, 2560], P('dp', 'sp'), parts along dimension 0
- output 2: bfloat16 [8, 4096, 2560], P('dp', 'sp'), parts along dimension 0
- output 3: bfloat16 [5120, 2048], P('dp'), parts along dimension 0
- output 4: bfloat16 [5120, 1024], P('dp'), parts along dimension 0
- output 5: bfloat16 [5120, 1024], P('dp'), parts along dimension 0
- output 6: bfloat16 [4096, 2560], P('dp'), parts along dimension 0
- output 7: float32 [5120], P('dp'), parts along dimension 0
- output 8: float32 [5120], P('dp'), parts along dimension 0
- output 9: float32 [512], P('dp'), parts along dimension 0
- output 10: float32 [512], P('dp'), parts along dimension 0
There are 2 independent parts. A program takes and returns all parts, laid end to end along the dimension named above; an argument that names none is the same for every part.
All inputs are finite; a program needn't handle non-finite values.
Results may differ from a plain program's by a relative error of at most 0.02.
Values are sent between devices in bfloat16 or wider.
A program may use at most 1 GiB of HBM per device.

v0:
```python
import functools
import jax
import jax.numpy as jnp
from jax import lax
from jax.sharding import PartitionSpec as P

EPS = 1e-6
ROPE_BASE = 1000000.0
ROPE_SCALE = 8.0
NEG_BIG = -1e30
Q_BLOCK = 1024


def rms_scale(x_f32, weight):
    inv_rms = lax.rsqrt(jnp.mean(x_f32 * x_f32, axis=-1, keepdims=True) + EPS)
    return x_f32 * inv_rms * (1.0 + weight)


def pre_norm(x_f32, weight):
    return rms_scale(x_f32, weight).astype(jnp.bfloat16)


def post_norm(proj, weight):
    return rms_scale(proj.astype(jnp.float32), weight)


def rope_tables(positions, head):
    half_dim = head // 2
    inv_freq = ROPE_BASE ** (-jnp.arange(half_dim, dtype=jnp.float32) * 2.0 / head)
    angles = (positions.astype(jnp.float32) / ROPE_SCALE)[:, None] * inv_freq[None, :]
    return jnp.cos(angles), jnp.sin(angles)


def norm_rope(heads_bf, weight, cosines, sines):
    half_dim = heads_bf.shape[-1] // 2
    normed = rms_scale(heads_bf.astype(jnp.float32), weight)
    first = normed[..., :half_dim]
    second = normed[..., half_dim:]
    cos_b = cosines[None, :, None, :]
    sin_b = sines[None, :, None, :]
    rotated = jnp.concatenate([first * cos_b - second * sin_b, second * cos_b + first * sin_b], axis=-1)
    return rotated.astype(jnp.bfloat16)


def causal_mask(start, block, end):
    row_ids = start + jnp.arange(block)
    col_ids = jnp.arange(end)
    return row_ids[:, None] >= col_ids[None, :]


def attention_fwd(q_all, k_all, v_all):
    batch, seq, q_heads, head = q_all.shape
    kv_loc = k_all.shape[2]
    scale = head ** -0.5
    block = min(Q_BLOCK, seq)
    q_grp = q_all.reshape(batch, seq, kv_loc, q_heads // kv_loc, head)
    pieces = []
    row_lse = []
    for index in range(seq // block):
        start = index * block
        end = start + block
        scores = jnp.einsum('bqkgh,bskh->bkgqs', q_grp[:, start:end], k_all[:, :end], preferred_element_type=jnp.float32) * scale
        scores = jnp.where(causal_mask(start, block, end), scores, NEG_BIG)
        row_max = jnp.max(scores, axis=-1, keepdims=True)
        exp_scores = jnp.exp(scores - row_max)
        row_sum = jnp.sum(exp_scores, axis=-1, keepdims=True)
        attn_prob = (exp_scores / row_sum).astype(jnp.bfloat16)
        pieces.append(jnp.einsum('bkgqs,bskh->bqkgh', attn_prob, v_all[:, :end], preferred_element_type=jnp.float32).astype(jnp.bfloat16))
        row_lse.append(row_max + jnp.log(row_sum))
    return jnp.concatenate(pieces, axis=1).reshape(batch, seq, q_heads, head), row_lse


def attention_bwd(q_all, k_all, v_all, row_lse, d_out):
    batch, seq, q_heads, head = q_all.shape
    kv_loc = k_all.shape[2]
    per_kv = q_heads // kv_loc
    scale = head ** -0.5
    block = min(Q_BLOCK, seq)
    q_grp = q_all.reshape(batch, seq, kv_loc, per_kv, head)
    do_grp = d_out.reshape(batch, seq, kv_loc, per_kv, head)
    dk_acc = jnp.zeros(k_all.shape, jnp.float32)
    dv_acc = jnp.zeros(v_all.shape, jnp.float32)
    dq_pieces = []
    for index in range(seq // block):
        start = index * block
        end = start + block
        q_blk = q_grp[:, start:end]
        do_blk = do_grp[:, start:end]
        k_pre = k_all[:, :end]
        v_pre = v_all[:, :end]
        scores = jnp.einsum('bqkgh,bskh->bkgqs', q_blk, k_pre, preferred_element_type=jnp.float32) * scale
        scores = jnp.where(causal_mask(start, block, end), scores, NEG_BIG)
        attn_prob = jnp.exp(scores - row_lse[index])
        d_prob = jnp.einsum('bqkgh,bskh->bkgqs', do_blk, v_pre, preferred_element_type=jnp.float32)
        d_score = (attn_prob * (d_prob - jnp.sum(d_prob * attn_prob, axis=-1, keepdims=True)) * scale).astype(jnp.bfloat16)
        dq_pieces.append(jnp.einsum('bkgqs,bskh->bqkgh', d_score, k_pre, preferred_element_type=jnp.float32).astype(jnp.bfloat16))
        dk_part = jnp.einsum('bkgqs,bqkgh->bskh', d_score, q_blk, preferred_element_type=jnp.float32)
        dv_part = jnp.einsum('bkgqs,bqkgh->bskh', attn_prob.astype(jnp.bfloat16), do_blk, preferred_element_type=jnp.float32)
        dk_acc = lax.dynamic_update_slice(dk_acc, dk_acc[:, :end] + dk_part, (0, 0, 0, 0))
        dv_acc = lax.dynamic_update_slice(dv_acc, dv_acc[:, :end] + dv_part, (0, 0, 0, 0))
    dq_all = jnp.concatenate(dq_pieces, axis=1).reshape(batch, seq, q_heads, head)
    return dq_all, dk_acc.astype(jnp.bfloat16), dv_acc.astype(jnp.bfloat16)


def fold_copies(grad_wide, kv_heads, rep):
    if rep == 1:
        return grad_wide
    batch, seq_loc, wide, head = grad_wide.shape
    summed = jnp.sum(grad_wide.reshape(batch, seq_loc, kv_heads, rep, head), axis=3, dtype=jnp.float32)
    return summed.astype(jnp.bfloat16)


def solution(mesh):
    group = mesh.shape['sp']

    def to_heads(arr):
        return lax.all_to_all(arr, 'sp', 2, 1, tiled=True)

    def to_tokens(arr):
        return lax.all_to_all(arr, 'sp', 1, 2, tiled=True)

    def device_step(x_in, dy_in, positions, w_q, w_k, w_v, w_o, w_pre, w_post, q_norm, k_norm):
        batch, seq_loc, width = x_in.shape
        head = q_norm.shape[0]
        heads = w_q.shape[1] // head
        kv_heads = w_k.shape[1] // head
        rep = max(1, group // kv_heads)
        x_f32 = x_in.astype(jnp.float32)
        normed, pre_pull = jax.vjp(pre_norm, x_f32, w_pre)
        q_proj = jnp.einsum('bsd,dn->bsn', normed, w_q, preferred_element_type=jnp.float32).astype(jnp.bfloat16).reshape(batch, seq_loc, heads, head)
        k_proj = jnp.einsum('bsd,dn->bsn', normed, w_k, preferred_element_type=jnp.float32).astype(jnp.bfloat16).reshape(batch, seq_loc, kv_heads, head)
        v_proj = jnp.einsum('bsd,dn->bsn', normed, w_v, preferred_element_type=jnp.float32).astype(jnp.bfloat16).reshape(batch, seq_loc, kv_heads, head)
        cosines, sines = rope_tables(positions, head)
        q_rot, q_pull = jax.vjp(functools.partial(norm_rope, cosines=cosines, sines=sines), q_proj, q_norm)
        k_rot, k_pull = jax.vjp(functools.partial(norm_rope, cosines=cosines, sines=sines), k_proj, k_norm)
        q_all = to_heads(q_rot)
        k_all = to_heads(jnp.repeat(k_rot, rep, axis=2))
        v_all = to_heads(jnp.repeat(v_proj, rep, axis=2))
        o_all, row_lse = attention_fwd(q_all, k_all, v_all)
        o_flat = to_tokens(o_all).reshape(batch, seq_loc, heads * head)
        proj = jnp.einsum('bsn,nd->bsd', o_flat, w_o, preferred_element_type=jnp.float32).astype(jnp.bfloat16)
        post, post_pull = jax.vjp(post_norm, proj, w_post)
        y_out = (x_f32 + post).astype(jnp.bfloat16)
        dy_f32 = dy_in.astype(jnp.float32)
        d_proj, dw_post = post_pull(dy_f32)
        dw_o = jnp.einsum('bsn,bsd->nd', o_flat, d_proj, preferred_element_type=jnp.float32)
        d_oflat = jnp.einsum('bsd,nd->bsn', d_proj, w_o, preferred_element_type=jnp.float32).astype(jnp.bfloat16)
        d_oall = to_heads(d_oflat.reshape(batch, seq_loc, heads, head))
        dq_all, dk_all, dv_all = attention_bwd(q_all, k_all, v_all, row_lse, d_oall)
        dq_rot = to_tokens(dq_all)
        dk_rot = fold_copies(to_tokens(dk_all), kv_heads, rep)
        dv_proj = fold_copies(to_tokens(dv_all), kv_heads, rep)
        dq_proj, dq_norm = q_pull(dq_rot)
        dk_proj, dk_norm = k_pull(dk_rot)
        dq_flat = dq_proj.reshape(batch, seq_loc, heads * head)
        dk_flat = dk_proj.reshape(batch, seq_loc, kv_heads * head)
        dv_flat = dv_proj.reshape(batch, seq_loc, kv_heads * head)
        dw_q = jnp.einsum('bsd,bsn->dn', normed, dq_flat, preferred_element_type=jnp.float32)
        dw_k = jnp.einsum('bsd,bsn->dn', normed, dk_flat, preferred_element_type=jnp.float32)
        dw_v = jnp.einsum('bsd,bsn->dn', normed, dv_flat, preferred_element_type=jnp.float32)
        d_normed = (jnp.einsum('bsn,dn->bsd', dq_flat, w_q, preferred_element_type=jnp.float32)
                    + jnp.einsum('bsn,dn->bsd', dk_flat, w_k, preferred_element_type=jnp.float32)
                    + jnp.einsum('bsn,dn->bsd', dv_flat, w_v, preferred_element_type=jnp.float32)).astype(jnp.bfloat16)
        dx_norm, dw_pre = pre_pull(d_normed)
        dx_out = (dy_f32 + dx_norm).astype(jnp.bfloat16)
        sums = lax.psum((dw_q, dw_k, dw_v, dw_o, dw_pre, dw_post, dq_norm, dk_norm), 'sp')
        return (y_out, dx_out, sums[0].astype(jnp.bfloat16), sums[1].astype(jnp.bfloat16), sums[2].astype(jnp.bfloat16), sums[3].astype(jnp.bfloat16), sums[4], sums[5], sums[6], sums[7])

    token_spec = P('dp', 'sp', None)
    return jax.shard_map(device_step, mesh=mesh,
                         in_specs=(token_spec, token_spec, P(('dp', 'sp')), P(None, None), P(None, None), P(None, None), P(None, None), P(None), P(None), P(None), P(None)),
                         out_specs=(token_spec, token_spec, P('dp', None), P('dp', None), P('dp', None), P('dp', None), P('dp'), P('dp'), P('dp'), P('dp')),
                         check_vma=False)
```

profile of v0, /device:TPU:1, one launch (start us, length us, event | category | flops | bytes accessed | tf_op | source)
XLA Modules:
  0.0 4087.4 jit_solution(4556302165397088305)
XLA Ops:
  129.4 53.4 %convert_convert_fusion = f32[4,1024,2048]{2,1,0:T(8,128)} fusion(bf16[2560,2048]{1,0:T(8,128)(2,1)} %param.14, bf16[4,1024,2560]{2,1,0:T(8,128)(2,1)} %param.11, f32[2560]{0:T(1024)S(1)} %broadcast_add_fusion.1, f32[4,1024]{1,0:T(4,128)S(1)} %fusion.114), kind=kOutput, calls=%fused_computation.131 | convolution fusion | flops 43008393216 | bytes 65038336 | tf_op jit(solution)/shard_map/bsd,dn->bsn/dot_general | solution.py:130
  233.5 31.9 copy.356
  397.7 123.6 %all-to-all-done.2 = bf16[4,1024,8,256]{3,1,0,2:T(8,128)(2,1)} async-done(((bf16[4,1024,8,256]{3,1,0,2:T(8,128)(2,1)}), bf16[4,1024,8,256]{3,1,0,2:T(8,128)(2,1)}, u32[]{:S(2)}, u32[]{:S(2)}) %all-to-all-start.2) | async-done | bytes 16777248 | tf_op jit(solution)/shard_map/all_to_all | solution.py:117
  657.2 38.3 fusion.125
  695.4 31.0 fusion.10
  726.4 38.0 convert_bitcast_fusion.6
  764.4 50.5 %fusion.124 = (f32[4,2,1024]{2,1,0:T(2,128)S(1)}, f32[4,1,2,1024,4096]{3,4,2,0,1:T(8,128)}) fusion(bf16[4,4096,256,1]{2,1,3,0:T(8,128)(2,1)} %bitcast.580, bf16[4,4096,1,2,256]{4,1,3,0,2:T(8,128)(2,1)} %bitcast.556, pred[1024,4096]{0,1:T(8,128)(4,1)} %iota_compare_fusion), kind=kOutput, calls=%fused_computation.227 | convolution fusion | flops 17280524288 | bytes 151027712 | tf_op jit(solution)/shard_map/bqkgh,bskh->bkgqs/dot_general | solution.py:62
  815.0 40.8 fusion.4
  855.8 47.2 %convert_bitcast_fusion.5 = bf16[4,1024,1,2,256]{1,4,3,0,2:T(8,128)(2,1)} fusion(f32[4,2,1024]{2,1,0:T(2,128)S(1)} %fusion.4, f32[4,1,2,1024,4096]{3,4,2,0,1:T(8,128)} %get-tuple-element.40, f32[4,2,1024]{2,1,0:T(2,128)S(1)} %get-tuple-element.39, bf16[4,4096,256,1]{1,2,0,3:T(8,128)(2,1)} %reshape.532), kind=kOutput, calls=%fused_computation.186 | convolution fusion | flops 17282629632 | bytes 146866176 | tf_op jit(solution)/shard_map/bkgqs,bskh->bqkgh/dot_general | solution.py:68
  916.7 40.9 copy.365
  966.1 181.8 %all-to-all-done.3 = bf16[4,4096,2,256]{3,2,0,1:T(2,128)(2,1)} async-done(((bf16[4,4096,2,256]{3,2,0,1:T(2,128)(2,1)}), bf16[4,4096,2,256]{3,2,0,1:T(2,128)(2,1)}, u32[]{:S(2)}, u32[]{:S(2)}) %all-to-all-start.3) | async-done | bytes 16777248 | tf_op jit(solution)/shard_map/all_to_all | solution.py:120
  1190.2 51.4 %fusion.41 = (f32[4,1024]{1,0:T(4,128)S(1)}, bf16[4,1024,2560]{2,1,0:T(8,128)(2,1)}) fusion(bf16[4,1024,2048]{2,1,0:T(8,128)(2,1)} %reshape.497, bf16[2048,2560]{1,0:T(8,128)(2,1)} %param.17), kind=kOutput, calls=%fused_computation.74 | convolution fusion | flops 42991611904 | bytes 48250880 | tf_op jit(solution)/shard_map/bsn,nd->bsd/dot_general | solution.py:141
  1271.5 52.1 %convolution_convert_fusion.1 = bf16[4,1024,2048]{2,1,0:T(8,128)(2,1)} fusion(bf16[2048,2560]{1,0:T(8,128)(2,1)} %param.17, bf16[4,1024,2560]{2,1,0:T(8,128)(2,1)} %param.12, bf16[4,1024,2560]{2,1,0:T(8,128)(2,1)} %get-tuple-element.48, f32[4,1024]{1,0:T(4,128)S(1)} %multiply_multiply_fusion.5, f32[2560]{0:T(1024)S(1)} %broadcast_add_fusion, ...), kind=kOutput, calls=%fused_computation.134 | convolution fusion | flops 43041947648 | bytes 69249024 | tf_op jit(solution)/shard_map/bsd,nd->bsn/dot_general | solution.py:147
  1358.8 56.5 %convolution_bitcast_fusion = f32[2048,2560]{1,0:T(8,128)} fusion(bf16[4,1024,2048]{2,1,0:T(8,128)(2,1)} %reshape.497, bf16[4,1024,2560]{2,1,0:T(8,128)(2,1)} %param.12, bf16[4,1024,2560]{2,1,0:T(8,128)(2,1)} %get-tuple-element.48, f32[4,1024]{1,0:T(4,128)S(1)} %multiply_multiply_fusion.5, f32[2560]{0:T(1024)S(1)} %broadcast_add_fusion, ...), kind=kOutput, calls=%fused_computation.135 | convolution fusion | flops 43033559040 | bytes 79734784 | tf_op jit(solution)/shard_map/bsn,bsd->nd/dot_general | solution.py:146
  1415.3 112.3 %all-to-all-done.4 = bf16[4,1024,8,256]{3,1,0,2:T(8,128)(2,1)} async-done(((bf16[4,1024,8,256]{3,1,0,2:T(8,128)(2,1)}), bf16[4,1024,8,256]{3,1,0,2:T(8,128)(2,1)}, u32[]{:S(2)}, u32[]{:S(2)}) %all-to-all-start.4) | async-done | bytes 16777248 | tf_op jit(solution)/shard_map/all_to_all | solution.py:117
  1584.0 49.3 %fusion.16 = (f32[4,2,1024]{2,1,0:T(2,128)}, f32[4,2048,1024,2]{2,1,3,0:T(8,128)}) fusion(f32[4,1,2,1024,2048]{3,4,2,0,1:T(8,128)} %get-tuple-element.44, f32[4,2,1024]{2,1,0:T(2,128)S(1)} %bitcast.588, bf16[4,4096,1,2,256]{4,1,3,0,2:T(8,128)(2,1)} %bitcast.546, bf16[4,4096,1,256]{1,3,0,2:T(8,128)(2,1)} %bitcast.567), kind=kOutput, calls=%fused_computation.39 | convolution fusion | flops 8640258048 | bytes 142671872 | tf_op jit(solution)/shard_map/bqkgh,bskh->bkgqs/dot_general | solution.py:94
  1673.8 68.6 %fusion.6 = (f32[4,2,1024]{2,1,0:T(2,128)}, f32[4,3072,1024,2]{2,1,3,0:T(8,128)}) fusion(f32[4,1,2,1024,3072]{3,4,2,0,1:T(8,128)} %get-tuple-element.42, f32[4,2,1024]{2,1,0:T(2,128)S(1)} %bitcast.594, bf16[4,4096,1,2,256]{4,1,3,0,2:T(8,128)(2,1)} %bitcast.548, bf16[4,4096,1,256]{1,3,0,2:T(8,128)(2,1)} %bitcast.568), kind=kOutput, calls=%fused_computation.15 | convolution fusion | flops 12960391168 | bytes 211877888 | tf_op jit(solution)/shard_map/bqkgh,bskh->bkgqs/dot_general | solution.py:94
  1742.4 44.4 %fusion.70 = f32[4,4096,1,256]{1,3,0,2:T(8,128)} fusion(f32[4,4096,1,256]{1,3,0,2:T(8,128)} %fusion.79, f32[4,1,2,1024,3072]{3,4,2,0,1:T(8,128)} %get-tuple-element.42, f32[4,2,1024]{2,1,0:T(2,128)S(1)} %bitcast.595, bf16[4,4096,1,2,256]{4,1,3,0,2:T(8,128)(2,1)} %bitcast.549), kind=kOutput, calls=%fused_computation.138 | convolution fusion | flops 12938379264 | bytes 130056192 | tf_op jit(solution)/shard_map/bkgqs,bqkgh->bskh/dot_general | solution.py:98
  1786.7 52.6 %fusion.65 = bf16[4,4096,1,256]{1,3,0,2:T(8,128)(2,1)} fusion(f32[4,4096,1,256]{1,3,0,2:T(8,128)} %fusion.70, f32[4,1,2,1024,4096]{3,4,2,0,1:T(8,128)} %get-tuple-element.40, f32[4,2,1024]{2,1,0:T(2,128)S(1)} %bitcast.591, bf16[4,4096,1,2,256]{4,1,3,0,2:T(8,128)(2,1)} %bitcast.550), kind=kOutput, calls=%fused_computation.115 | convolution fusion | flops 17255366656 | bytes 163610624 | tf_op jit(solution)/shard_map/bkgqs,bqkgh->bskh/dot_general | solution.py:98
  1908.7 78.6 %fusion.28 = bf16[4,2,1024,3072]{2,3,1,0:T(8,128)(2,1)} fusion(f32[4,3072,1024,2]{2,1,3,0:T(8,128)} %get-tuple-element.52, f32[4,1,2,1024,3072]{3,4,2,0,1:T(8,128)} %get-tuple-element.42, f32[4,2,1024]{2,1,0:T(2,128)S(1)} %copy-done.43, f32[4,2,1024]{2,1,0:T(2,128)S(1)} %bitcast.596), kind=kLoop, calls=%fused_computation.60 | loop fusion | flops 125829120 | bytes 251723776 | tf_op jit(solution)/shard_map/reshape.88
  2011.1 53.5 %fusion.50 = bf16[4,2,1024,2048]{2,3,1,0:T(8,128)(2,1)} fusion(f32[4,2048,1024,2]{2,1,3,0:T(8,128)} %get-tuple-element.54, f32[4,1,2,1024,2048]{3,4,2,0,1:T(8,128)} %get-tuple-element.44, f32[4,2,1024]{2,1,0:T(2,128)S(1)} %copy-done.33, f32[4,2,1024]{2,1,0:T(2,128)S(1)} %bitcast.590), kind=kLoop, calls=%fused_computation.83 | loop fusion | flops 83886080 | bytes 167837696 | tf_op jit(solution)/shard_map/reshape.80
  2114.5 88.9 %fusion = (f32[4,2,1024]{2,1,0:T(2,128)S(1)}, f32[4,4096,1024,2]{2,1,3,0:T(8,128)}) fusion(f32[4,1,2,1024,4096]{3,4,2,0,1:T(8,128)} %get-tuple-element.40, f32[4,2,1024]{2,1,0:T(2,128)S(1)} %bitcast.592, bf16[4,4096,256,1]{2,1,3,0:T(8,128)(2,1)} %bitcast.569, bf16[4,4096,1,2,256]{4,1,3,0,2:T(8,128)(2,1)} %bitcast.551), kind=kOutput, calls=%fused_computation.3 | convolution fusion | flops 17280524288 | bytes 281083904 | tf_op jit(solution)/shard_map/bqkgh,bskh->bkgqs/dot_general | solution.py:94
  2203.4 104.5 %fusion.15 = bf16[4,2,1024,4096]{2,3,1,0:T(8,128)(2,1)} fusion(f32[4,4096,1024,2]{2,1,3,0:T(8,128)} %get-tuple-element.50, f32[4,1,2,1024,4096]{3,4,2,0,1:T(8,128)} %get-tuple-element.40, f32[4,2,1024]{2,1,0:T(2,128)S(1)} %get-tuple-element.49, f32[4,2,1024]{2,1,0:T(2,128)S(1)} %bitcast.593), kind=kLoop, calls=%fused_computation.35 | loop fusion | flops 167772160 | bytes 335609856 | tf_op jit(solution)/shard_map/reshape.96
  2307.9 34.7 fusion.66
  2432.5 41.1 %copy.381 = bf16[4,4096,2,256]{3,2,0,1:T(2,128)(2,1)} copy(bf16[4,4096,2,256]{1,3,2,0:T(8,128)(2,1)} %maximum_bitcast_fusion.1) | data formatting | bytes 33554432 | tf_op jit(solution)/shard_map/reshape | solution.py:101
  2599.5 31.9 convolution_bitcast_fusion.3
  2659.9 59.0 %all-to-all-done.5 = bf16[4,4096,2,256]{3,2,0,1:T(2,128)(2,1)} async-done(((bf16[4,4096,2,256]{3,2,0,1:T(2,128)(2,1)}), bf16[4,4096,2,256]{3,2,0,1:T(2,128)(2,1)}, u32[]{:S(2)}, u32[]{:S(2)}) %all-to-all-start.5) | async-done | bytes 16777248 | tf_op jit(solution)/shard_map/all_to_all | solution.py:120
  2718.9 45.4 %copy.382 = f32[4,4,1024,2,256]{2,4,3,1,0:T(8,128)} copy(bf16[4,4,1024,2,256]{4,3,0,2,1:T(2,128)(2,1)} %bitcast.198) | data formatting | bytes 50331648 | tf_op jit(solution)/shard_map/transpose(jvp())/convert_element_type | solution.py:42
  2837.7 57.4 %convolution_bitcast_fusion.1 = f32[2560,2048]{1,0:T(8,128)} fusion(bf16[4,1024,2048]{1,2,0:T(8,128)(2,1)} %bitcast.574, bf16[4,1024,2560]{2,1,0:T(8,128)(2,1)} %param.11, f32[2560]{0:T(1024)S(1)} %copy-done.51, f32[4,1024]{1,0:T(4,128)S(1)} %copy-done.49), kind=kOutput, calls=%fused_computation.136 | convolution fusion | flops 42991616000 | bytes 58746880 | tf_op jit(solution)/shard_map/bsd,bsn->dn/dot_general | solution.py:158
  2895.1 53.7 %fusion.74 = f32[4,1024,2560]{2,1,0:T(8,128)} fusion(bf16[4,1024,2048]{1,2,0:T(8,128)(2,1)} %bitcast.575, bf16[2560,2048]{1,0:T(8,128)(2,1)} %param.14), kind=kOutput, calls=%fused_computation.144 | convolution fusion | flops 42949672960 | bytes 69206016 | tf_op jit(solution)/shard_map/bsn,dn->bsd/dot_general | solution.py:161
  2948.8 49.2 %fusion.37 = (f32[2560]{0:T(1024)S(1)}, f32[4,1024]{1,0:T(4,128)S(1)}, bf16[4,1024,2560]{2,1,0:T(8,128)(2,1)}) fusion(bf16[4,1024,2560]{2,1,0:T(8,128)(2,1)} %param.11, f32[4,1024]{1,0:T(4,128)S(1)} %copy-done.49, f32[2560]{0:T(1024)S(1)} %copy-done.51, bf16[4,1024,1024]{2,1,0:T(8,128)(2,1)} %reshape.515, bf16[2560,1024]{1,0:T(8,128)(2,1)} %param.16, ...), kind=kOutput, calls=%fused_computation.70 | convolution fusion | flops 21590173696 | bytes 139513856 | tf_op jit(solution)/shard_map/bsn,dn->bsd/dot_general | solution.py:163
  3026.4 1060.8 %all-reduce.8 = (bf16[2560,2048]{1,0:T(8,128)(2,1)}, bf16[2560,1024]{1,0:T(8,128)(2,1)}, bf16[2560,1024]{1,0:T(8,128)(2,1)}, bf16[2048,2560]{1,0:T(8,128)(2,1)},...) all-reduce(f32[2560,2048]{1,0:T(8,128)} %convolution_bitcast_fusion, ...), channel_id=1, replica_groups=mesh['dp'=2,'sp'=4] {'sp'}, use_global_device_ids=true, to_apply=%region_20.21 | all-reduce | flops 15734272 | bytes 94416896 | tf_op jit(solution)/shard_map/psum | solution.py:166
  (249 shorter events, 1162.4 us)
Async XLA Ops:
  1.5 127.8 %copy-start.50 = (f32[2560]{0:T(1024)}, f32[2560]{0:T(1024)S(1)}, u32[]{:S(2)}) copy-start(f32[2560]{0:T(1024)S(1)} %broadcast_add_fusion.1) | copy-start | bytes 30724
  11.6 117.8 %copy-start.48 = (f32[4,1024]{1,0:T(4,128)}, f32[4,1024]{1,0:T(4,128)S(1)}, u32[]{:S(2)}) copy-start(f32[4,1024]{1,0:T(4,128)S(1)} %fusion.114) | copy-start | bytes 49156
  48.5 164.1 %all-to-all-start = ((bf16[4,1024,4,256]{1,3,0,2:T(8,128)(2,1)}), bf16[4,1024,4,256]{1,3,0,2:T(8,128)(2,1)}, u32[]{:S(2)}, u32[]{:S(2)}) async-start(bf16[4,1024,4,256]{1,3,0,2:T(8,128)(2,1)} %copy.347), calls=%async_computation | async-start | bytes 16777216 | tf_op jit(solution)/shard_map/all_to_all | solution.py:117
  54.3 45.6 %copy-start.53 = (f32[256]{0:T(256)}, f32[256]{0:T(256)S(1)}, u32[]{:S(2)}) copy-start(f32[256]{0:T(256)S(1)} %broadcast_add_fusion.3) | copy-start | bytes 3076
  56.3 30.4 copy-start
  56.3 30.4 copy-start.3
  56.5 51.3 %copy-start.6 = (f32[1024,128]{1,0:T(8,128)}, f32[1024,128]{1,0:T(8,128)S(1)}, u32[]{:S(2)}) copy-start(f32[1024,128]{1,0:T(8,128)S(1)} %copy.351) | copy-start | bytes 1572868
  56.7 51.1 %copy-start.7 = (f32[1024,128]{1,0:T(8,128)}, f32[1024,128]{1,0:T(8,128)S(1)}, u32[]{:S(2)}) copy-start(f32[1024,128]{1,0:T(8,128)S(1)} %copy.352) | copy-start | bytes 1572868
  212.6 119.3 %all-to-all-start.1 = ((bf16[4,1024,4,256]{1,3,0,2:T(8,128)(2,1)}), bf16[4,1024,4,256]{1,3,0,2:T(8,128)(2,1)}, u32[]{:S(2)}, u32[]{:S(2)}) async-start(bf16[4,1024,4,256]{1,3,0,2:T(8,128)(2,1)} %copy.353), calls=%async_computation.1 | async-start | bytes 16777216 | tf_op jit(solution)/shard_map/all_to_all | solution.py:117
  233.5 31.9 copy-start.16
  233.5 31.9 copy-start.62
  331.8 189.5 %all-to-all-start.2 = ((bf16[4,1024,8,256]{3,1,0,2:T(8,128)(2,1)}), bf16[4,1024,8,256]{3,1,0,2:T(8,128)(2,1)}, u32[]{:S(2)}, u32[]{:S(2)}) async-start(bf16[4,1024,8,256]{3,1,0,2:T(8,128)(2,1)} %copy.357), calls=%async_computation.2 | async-start | bytes 33554432 | tf_op jit(solution)/shard_map/all_to_all | solution.py:117
  550.9 41.0 %copy-start.39 = (f32[4,2,1024]{2,1,0:T(2,128)}, f32[4,2,1024]{2,1,0:T(2,128)S(1)}, u32[]{:S(2)}) copy-start(f32[4,2,1024]{2,1,0:T(2,128)S(1)} %get-tuple-element.45) | copy-start | bytes 98308
  578.7 50.9 %copy-start.29 = (f32[4,2,1024]{2,1,0:T(2,128)}, f32[4,2,1024]{2,1,0:T(2,128)S(1)}, u32[]{:S(2)}) copy-start(f32[4,2,1024]{2,1,0:T(2,128)S(1)} %get-tuple-element.43) | copy-start | bytes 98308
  695.4 31.0 copy-start.35
  726.4 38.0 copy-start.37
  815.0 40.8 copy-start.44
  855.8 47.2 %copy-start.46 = (f32[4,2,1024]{2,1,0:T(2,128)}, f32[4,2,1024]{2,1,0:T(2,128)S(1)}, u32[]{:S(2)}) copy-start(f32[4,2,1024]{2,1,0:T(2,128)S(1)} %fusion.4) | copy-start | bytes 98308
  957.6 190.3 %all-to-all-start.3 = ((bf16[4,4096,2,256]{3,2,0,1:T(2,128)(2,1)}), bf16[4,4096,2,256]{3,2,0,1:T(2,128)(2,1)}, u32[]{:S(2)}, u32[]{:S(2)}) async-start(bf16[4,4096,2,256]{3,2,0,1:T(2,128)(2,1)} %copy.365), calls=%async_computation.3 | async-start | bytes 33554432 | tf_op jit(solution)/shard_map/all_to_all | solution.py:120
  1337.4 190.2 %all-to-all-start.4 = ((bf16[4,1024,8,256]{3,1,0,2:T(8,128)(2,1)}), bf16[4,1024,8,256]{3,1,0,2:T(8,128)(2,1)}, u32[]{:S(2)}, u32[]{:S(2)}) async-start(bf16[4,1024,8,256]{3,1,0,2:T(8,128)(2,1)} %bitcast.561), calls=%async_computation.4 | async-start | bytes 33554432 | tf_op jit(solution)/shard_map/all_to_all | solution.py:117
  1357.5 201.4 %copy-start.23 = (f32[1,8,1024]{2,1,0:T(8,128)}, f32[1,8,1024]{2,1,0:T(8,128)S(1)}, u32[]{:S(2)}) copy-start(f32[1,8,1024]{2,1,0:T(8,128)S(1)} %log_add_fusion.3) | copy-start | bytes 98308
  1357.5 285.9 %copy-start.14 = (f32[1,8,1024]{2,1,0:T(8,128)}, f32[1,8,1024]{2,1,0:T(8,128)S(1)}, u32[]{:S(2)}) copy-start(f32[1,8,1024]{2,1,0:T(8,128)S(1)} %log_add_fusion.2) | copy-start | bytes 98308
  1643.4 30.4 copy-start.22
  1742.4 44.4 %copy-start.20 = (f32[1,8,1024]{2,1,0:T(8,128)S(1)}, f32[1,8,1024]{2,1,0:T(8,128)}, u32[]{:S(2)}) copy-start(f32[1,8,1024]{2,1,0:T(8,128)} %log_add_fusion) | copy-start | bytes 98308
  1853.0 551.1 %all-to-all-start.7 = ((bf16[4,4096,1,256]{3,0,2,1:T(4,128)(2,1)}), bf16[4,4096,1,256]{3,0,2,1:T(4,128)(2,1)}, u32[]{:S(2)}, u32[]{:S(2)}) async-start(bf16[4,4096,1,256]{3,0,2,1:T(4,128)(2,1)} %copy.408), calls=%async_computation.7 | async-start | bytes 16777216 | tf_op jit(solution)/shard_map/all_to_all | solution.py:120
  2404.0 125.8 %all-to-all-start.6 = ((bf16[4,4096,1,256]{3,0,2,1:T(4,128)(2,1)}), bf16[4,4096,1,256]{3,0,2,1:T(4,128)(2,1)}, u32[]{:S(2)}, u32[]{:S(2)}) async-start(bf16[4,4096,1,256]{3,0,2,1:T(4,128)(2,1)} %copy.394), calls=%async_computation.6 | async-start | bytes 16777216 | tf_op jit(solution)/shard_map/all_to_all | solution.py:120
  2529.8 189.1 %all-to-all-start.5 = ((bf16[4,4096,2,256]{3,2,0,1:T(2,128)(2,1)}), bf16[4,4096,2,256]{3,2,0,1:T(2,128)(2,1)}, u32[]{:S(2)}, u32[]{:S(2)}) async-start(bf16[4,4096,2,256]{3,2,0,1:T(2,128)(2,1)} %copy.381), calls=%async_computation.5 | async-start | bytes 33554432 | tf_op jit(solution)/shard_map/all_to_all | solution.py:120
  2588.1 43.4 %slice-start.4 = ((s8[5242880]{0:T(1024)(128)(4,1)}), s8[1048576]{0:T(1024)(128)(4,1)S(1)}, s32[]{:S(2)}) async-start(s8[5242880]{0:T(1024)(128)(4,1)} %bitcast.608), calls=%async_computation.12 | async-start | bytes 2097152
  2599.5 31.9 slice-start.5
  2718.9 45.4 %copy-start.2 = (f32[1024,128]{0,1:T(8,128)S(1)}, f32[1024,128]{0,1:T(8,128)}, u32[]{:S(2)}) copy-start(f32[1024,128]{0,1:T(8,128)} %copy-done) | copy-start | bytes 1572868
  2718.9 45.4 %copy-start.5 = (f32[1024,128]{0,1:T(8,128)S(1)}, f32[1024,128]{0,1:T(8,128)}, u32[]{:S(2)}) copy-start(f32[1024,128]{0,1:T(8,128)} %copy-done.3) | copy-start | bytes 1572868
  2948.8 49.2 %copy-start.28 = (f32[4,1024]{1,0:T(4,128)S(1)}, f32[4,1024]{1,0:T(4,128)}, u32[]{:S(2)}) copy-start(f32[4,1024]{1,0:T(4,128)} %copy-done.27) | copy-start | bytes 49156
  (47 other events, 807.1 us)
where the time goes:
time: 4100 us; the launch traced here: 4090 us
  matrix products  1340 us (33%)
  blocking collectives  1060 us (26%)
  other arithmetic  670 us (16%)
  local copies, waits for them, and re-layouts  481 us (12%)
  waiting for transfers between devices  477 us (12%)
  starting transfers between devices  55.6 us (1%)
    psum x1, blocking collectives, device_step(): lax.psum((dw_q, dw_k, dw_v, dw_o, dw_pre, dw_post, dq_norm, dk_norm), 'sp')  1060 us
    another operation x6, other arithmetic  280 us
    all_to_all x4, waiting for transfers between devices, to_tokens(): return lax.all_to_all(arr, 'sp', 1, 2, tiled=True)  241 us
    all_to_all x4, waiting for transfers between devices, to_heads(): return lax.all_to_all(arr, 'sp', 2, 1, tiled=True)  236 us
    dot_general x4, matrix products, attention_bwd(): jnp.einsum('bqkgh,bskh->bkgqs', do_blk, v_pre, preferred_element_type=jnp...  232 us
    dot_general x4, matrix products, attention_bwd(): jnp.einsum('bkgqs,bqkgh->bskh', attn_prob.astype(jnp.bfloat16), do_blk, p...  145 us
    dot_general x4, matrix products, attention_fwd(): jnp.einsum('bqkgh,bskh->bkgqs', q_grp[:, start:end], k_all[:, :end], pref...  132 us
    dot_general x4, matrix products, attention_fwd(): jnp.einsum('bkgqs,bskh->bqkgh', attn_prob, v_all[:, :end], preferred_elem...  129 us
  transfers between devices with their start and end apart: 8, of which 4 were waited for; matrix products, arithmetic and copies ran while one was open for 29% of the time, Pallas kernels for 0%

commit v1 on v0

v1 whole, which is shorter than its diff:
```python
import functools
import math
import jax
import jax.numpy as jnp
from jax import lax
from jax.experimental import pallas as pl
from jax.experimental.pallas import tpu as pltpu
from jax.sharding import PartitionSpec as P

EPS = 1e-6
ROPE_BASE = 1000000.0
ROPE_SCALE = 8.0
NEG_BIG = -1e30
LOG2E = math.log2(math.e)
BLOCK = 512
NORM_BLOCK = 256
VMEM_LIMIT = 60 * 1024 * 1024

NT = (((1,), (1,)), ((), ()))
NN = (((1,), (0,)), ((), ()))


def dot(lhs, rhs, dims=NN):
    return lax.dot_general(lhs, rhs, dims, preferred_element_type=jnp.float32)


def row_call(body, toks, rows_in, vecs, rows_out, acc_width, flops):
    rows = lambda arr: pl.BlockSpec((NORM_BLOCK, arr.shape[1]), lambda i: (i, 0))
    vec = lambda arr: pl.BlockSpec((1, arr.shape[1]), lambda i: (0, 0))
    out_specs = [rows(arr) for arr in rows_out]
    out_shape = list(rows_out)
    if acc_width:
        out_specs.append(pl.BlockSpec((8, acc_width), lambda i: (0, 0)))
        out_shape.append(jax.ShapeDtypeStruct((8, acc_width), jnp.float32))
    moved = sum(arr.size * arr.dtype.itemsize for arr in list(rows_in) + list(rows_out))
    return pl.pallas_call(
        body,
        grid=(toks // NORM_BLOCK,),
        in_specs=[rows(arr) for arr in rows_in] + [vec(arr) for arr in vecs],
        out_specs=out_specs,
        out_shape=out_shape,
        compiler_params=pltpu.CompilerParams(dimension_semantics=('arbitrary',), vmem_limit_bytes=VMEM_LIMIT),
        cost_estimate=pl.CostEstimate(flops=flops, bytes_accessed=moved, transcendentals=0),
    )(*rows_in, *vecs)


def pre_norm_kernel(x_ref, w_ref, a_ref):
    x = x_ref[...].astype(jnp.float32)
    inv = lax.rsqrt(jnp.mean(x * x, axis=-1, keepdims=True) + EPS)
    a_ref[...] = (x * inv * (1.0 + w_ref[...])).astype(jnp.bfloat16)


def fold_rows(arr):
    return jnp.sum(arr.reshape(-1, 8, arr.shape[1]), axis=0)


def post_norm_kernel(x_ref, proj_ref, dy_ref, w_ref, y_ref, dproj_ref, dw_ref):
    @pl.when(pl.program_id(0) == 0)
    def _():
        dw_ref[...] = jnp.zeros_like(dw_ref)

    gain = 1.0 + w_ref[...]
    proj = proj_ref[...].astype(jnp.float32)
    inv = lax.rsqrt(jnp.mean(proj * proj, axis=-1, keepdims=True) + EPS)
    hat = proj * inv
    y_ref[...] = (x_ref[...].astype(jnp.float32) + hat * gain).astype(jnp.bfloat16)
    dy = dy_ref[...].astype(jnp.float32)
    dw_ref[...] += fold_rows(dy * hat)
    grad = dy * gain
    mean = jnp.mean(grad * hat, axis=-1, keepdims=True)
    dproj_ref[...] = ((grad - hat * mean) * inv).astype(jnp.bfloat16)


def pre_norm_bwd_kernel(x_ref, dn_ref, dy_ref, w_ref, dx_ref, dw_ref):
    @pl.when(pl.program_id(0) == 0)
    def _():
        dw_ref[...] = jnp.zeros_like(dw_ref)

    x = x_ref[...].astype(jnp.float32)
    inv = lax.rsqrt(jnp.mean(x * x, axis=-1, keepdims=True) + EPS)
    hat = x * inv
    grad = dn_ref[...].astype(jnp.float32)
    dw_ref[...] += fold_rows(grad * hat)
    grad = grad * (1.0 + w_ref[...])
    mean = jnp.mean(grad * hat, axis=-1, keepdims=True)
    dx_ref[...] = (dy_ref[...].astype(jnp.float32) + (grad - hat * mean) * inv).astype(jnp.bfloat16)


def like(arr):
    return jax.ShapeDtypeStruct(arr.shape, jnp.bfloat16)


def rope_tables(positions, head):
    half_dim = head // 2
    inv_freq = ROPE_BASE ** (-jnp.arange(half_dim, dtype=jnp.float32) * 2.0 / head)
    angles = (positions.astype(jnp.float32) / ROPE_SCALE)[:, None] * inv_freq[None, :]
    return jnp.cos(angles), jnp.sin(angles)


def norm_rope_kernel(q_ref, k_ref, cos_ref, sin_ref, qn_ref, kn_ref, qo_ref, ko_ref, *, head):
    half = head // 2
    cos = cos_ref[...]
    sin = sin_ref[...]
    for src, weight, dst in ((q_ref, qn_ref, qo_ref), (k_ref, kn_ref, ko_ref)):
        gain = 1.0 + weight[...]
        for h in range(src.shape[1] // head):
            x = src[:, h * head:(h + 1) * head].astype(jnp.float32)
            inv = lax.rsqrt(jnp.mean(x * x, axis=-1, keepdims=True) + EPS)
            n = x * inv * gain
            a, b = n[:, :half], n[:, half:]
            dst[:, h * head:h * head + half] = (a * cos - b * sin).astype(jnp.bfloat16)
            dst[:, h * head + half:(h + 1) * head] = (b * cos + a * sin).astype(jnp.bfloat16)


def norm_rope(q, k, cos, sin, q_norm, k_norm, head):
    toks = q.shape[0]
    rows = lambda width: pl.BlockSpec((NORM_BLOCK, width), lambda i: (i, 0))
    whole = pl.BlockSpec((1, head), lambda i: (0, 0))
    return pl.pallas_call(
        functools.partial(norm_rope_kernel, head=head),
        grid=(toks // NORM_BLOCK,),
        in_specs=[rows(q.shape[1]), rows(k.shape[1]), rows(head // 2), rows(head // 2), whole, whole],
        out_specs=[rows(q.shape[1]), rows(k.shape[1])],
        out_shape=[jax.ShapeDtypeStruct(q.shape, jnp.bfloat16), jax.ShapeDtypeStruct(k.shape, jnp.bfloat16)],
        compiler_params=pltpu.CompilerParams(dimension_semantics=('arbitrary',), vmem_limit_bytes=VMEM_LIMIT),
        cost_estimate=pl.CostEstimate(flops=(q.size + k.size) * 200, bytes_accessed=(q.size + k.size) * 4, transcendentals=0),
        name='norm_rope',
    )(q, k, cos, sin, q_norm.reshape(1, head), k_norm.reshape(1, head))


def norm_rope_bwd_kernel(dq_ref, dk_ref, q_ref, k_ref, cos_ref, sin_ref, qn_ref, kn_ref, dqo_ref, dko_ref, dqn_ref, dkn_ref, *, head):
    half = head // 2
    cos = cos_ref[...]
    sin = sin_ref[...]

    @pl.when(pl.program_id(0) == 0)
    def _():
        dqn_ref[...] = jnp.zeros_like(dqn_ref)
        dkn_ref[...] = jnp.zeros_like(dkn_ref)

    for grad, src, weight, dst, dwn in ((dq_ref, q_ref, qn_ref, dqo_ref, dqn_ref), (dk_ref, k_ref, kn_ref, dko_ref, dkn_ref)):
        gain = 1.0 + weight[...]
        dw_a = jnp.zeros((8, half), jnp.float32)
        dw_b = jnp.zeros((8, half), jnp.float32)
        for h in range(src.shape[1] // head):
            lo = slice(h * head, h * head + half)
            hi = slice(h * head + half, (h + 1) * head)
            xa = src[:, lo].astype(jnp.float32)
            xb = src[:, hi].astype(jnp.float32)
            ga = grad[:, lo].astype(jnp.float32)
            gb = grad[:, hi].astype(jnp.float32)
            inv = lax.rsqrt(jnp.sum(xa * xa + xb * xb, axis=-1, keepdims=True) / head + EPS)
            na = ga * cos + gb * sin
            nb = gb * cos - ga * sin
            xa = xa * inv
            xb = xb * inv
            dw_a = dw_a + jnp.sum((na * xa).reshape(-1, 8, half), axis=0)
            dw_b = dw_b + jnp.sum((nb * xb).reshape(-1, 8, half), axis=0)
            na = na * gain[:, :half]
            nb = nb * gain[:, half:]
            mean = jnp.sum(na * xa + nb * xb, axis=-1, keepdims=True) / head
            dst[:, lo] = ((na - xa * mean) * inv).astype(jnp.bfloat16)
            dst[:, hi] = ((nb - xb * mean) * inv).astype(jnp.bfloat16)
        dwn[:, :half] += dw_a
        dwn[:, half:] += dw_b


def norm_rope_bwd(dq, dk, q, k, cos, sin, q_norm, k_norm, head):
    toks = q.shape[0]
    rows = lambda width: pl.BlockSpec((NORM_BLOCK, width), lambda i: (i, 0))
    whole = pl.BlockSpec((1, head), lambda i: (0, 0))
    acc = pl.BlockSpec((8, head), lambda i: (0, 0))
    dq_o, dk_o, dqn, dkn = pl.pallas_call(
        functools.partial(norm_rope_bwd_kernel, head=head),
        grid=(toks // NORM_BLOCK,),
        in_specs=[rows(q.shape[1]), rows(k.shape[1]), rows(q.shape[1]), rows(k.shape[1]), rows(head // 2), rows(head // 2), whole, whole],
        out_specs=[rows(q.shape[1]), rows(k.shape[1]), acc, acc],
        out_shape=[jax.ShapeDtypeStruct(q.shape, jnp.bfloat16), jax.ShapeDtypeStruct(k.shape, jnp.bfloat16),
                   jax.ShapeDtypeStruct((8, head), jnp.float32), jax.ShapeDtypeStruct((8, head), jnp.float32)],
        compiler_params=pltpu.CompilerParams(dimension_semantics=('arbitrary',), vmem_limit_bytes=VMEM_LIMIT),
        cost_estimate=pl.CostEstimate(flops=(q.size + k.size) * 300, bytes_accessed=(q.size + k.size) * 6, transcendentals=0),
        name='norm_rope_bwd',
    )(dq, dk, q, k, cos, sin, q_norm.reshape(1, head), k_norm.reshape(1, head))
    return dq_o, dk_o, jnp.sum(dqn, axis=0), jnp.sum(dkn, axis=0)


def causal_tile(scores):
    keys = lax.broadcasted_iota(jnp.int32, scores.shape, 0)
    queries = lax.broadcasted_iota(jnp.int32, scores.shape, 1)
    return jnp.where(queries >= keys, scores, NEG_BIG)


def attn_fwd_kernel(q_ref, k_ref, v_ref, o_ref, lse_ref, vt_ref, acc_ref, *, head, per_kv):
    i = pl.program_id(1)
    blk = BLOCK
    c = LOG2E * head ** -0.5

    @pl.when(i == 0)
    def _():
        for t in range(v_ref.shape[0] // blk):
            vt_ref[:, t * blk:(t + 1) * blk] = v_ref[t * blk:(t + 1) * blk, :].astype(jnp.float32).T.astype(jnp.bfloat16)

    qs = [q_ref[:, g * head:(g + 1) * head] for g in range(per_kv)]

    def tile(j, carry, masked, first):
        start = pl.multiple_of(j * blk, blk)
        k_blk = k_ref[pl.ds(start, blk), :]
        vt_blk = vt_ref[:, pl.ds(start, blk)]
        out = []
        scores = [dot(k_blk, qs[g], NT) for g in range(per_kv)]
        if masked:
            scores = [causal_tile(s) for s in scores]
        for g in range(per_kv):
            s = scores[g]
            top = jnp.max(s, axis=0, keepdims=True)
            if not first:
                m_old, l_old = carry[g]
                top = jnp.maximum(top, m_old)
            p = jnp.exp2(s * c - top * c)
            total = jnp.sum(p, axis=0, keepdims=True)
            pv = dot(vt_blk, p.astype(jnp.bfloat16))
            if first:
                acc_ref[g] = pv
            else:
                alpha = jnp.exp2((m_old - top) * c)
                total = total + l_old * alpha
                acc_ref[g] = acc_ref[g] * alpha + pv
            out.append((top, total))
        return tuple(out)

    state = tile(i, None, True, True)
    state = lax.fori_loop(0, i, lambda j, st: tile(j, st, False, False), state)
    for g in range(per_kv):
        top, total = state[g]
        o_ref[:, g * head:(g + 1) * head] = (acc_ref[g] * (1.0 / total)).T.astype(jnp.bfloat16)
        lse_ref[0, g:g + 1, :] = top * c + jnp.log2(total)


def attn_fwd(q, k, v, head):
    toks = q.shape[0]
    kv_heads = k.shape[1] // head
    per_kv = q.shape[1] // k.shape[1]
    wide = per_kv * head
    blocks = toks // BLOCK
    flops = 2 * 2 * toks * toks // 2 * q.shape[1]
    return pl.pallas_call(
        functools.partial(attn_fwd_kernel, head=head, per_kv=per_kv),
        grid=(kv_heads, blocks),
        in_specs=[pl.BlockSpec((BLOCK, wide), lambda h, i: (i, h)),
                  pl.BlockSpec((toks, head), lambda h, i: (0, h)),
                  pl.BlockSpec((toks, head), lambda h, i: (0, h))],
        out_specs=[pl.BlockSpec((BLOCK, wide), lambda h, i: (i, h)),
                   pl.BlockSpec((1, per_kv, BLOCK), lambda h, i: (h, 0, i))],
        out_shape=[jax.ShapeDtypeStruct(q.shape, jnp.bfloat16),
                   jax.ShapeDtypeStruct((kv_heads, per_kv, toks), jnp.float32)],
        scratch_shapes=[pltpu.VMEM((head, toks), jnp.bfloat16), pltpu.VMEM((per_kv, head, BLOCK), jnp.float32)],
        compiler_params=pltpu.CompilerParams(dimension_semantics=('arbitrary', 'arbitrary'), vmem_limit_bytes=VMEM_LIMIT),
        cost_estimate=pl.CostEstimate(flops=2 * flops, bytes_accessed=(q.size + k.size) * 4, transcendentals=0),
        name='attn_fwd',
    )(q, k, v)


def delta_kernel(o_ref, do_ref, delta_ref, *, head, per_kv):
    half = head // 2
    for g in range(per_kv):
        prod = o_ref[:, g * head:(g + 1) * head].astype(jnp.float32) * do_ref[:, g * head:(g + 1) * head].astype(jnp.float32)
        delta_ref[0, g:g + 1, :] = jnp.sum((prod[:, :half] + prod[:, half:]).T, axis=0, keepdims=True)


def attn_delta(o, d_out, kv_heads, head):
    toks, width = o.shape
    wide = width // kv_heads
    rows = min(toks, 1024)
    spec = pl.BlockSpec((rows, wide), lambda h, i: (i, h))
    return pl.pallas_call(
        functools.partial(delta_kernel, head=head, per_kv=wide // head),
        grid=(kv_heads, toks // rows),
        in_specs=[spec, spec],
        out_specs=pl.BlockSpec((1, wide // head, rows), lambda h, i: (h, 0, i)),
        out_shape=jax.ShapeDtypeStruct((kv_heads, wide // head, toks), jnp.float32),
        compiler_params=pltpu.CompilerParams(dimension_semantics=('arbitrary', 'arbitrary'), vmem_limit_bytes=VMEM_LIMIT),
        cost_estimate=pl.CostEstimate(flops=o.size * 200, bytes_accessed=o.size * 4, transcendentals=0),
        name='attn_delta',
    )(o, d_out)


def attn_bwd_kernel(q_ref, do_ref, lse_ref, delta_ref, k_ref, v_ref, dq_ref, dk_ref, dv_ref, dqt_ref, dk_acc, dv_acc, *, head, per_kv, blocks):
    j = pl.program_id(1)
    blk = BLOCK
    scale = head ** -0.5
    c = LOG2E * scale

    @pl.when(j == 0)
    def _():
        dqt_ref[...] = jnp.zeros_like(dqt_ref)

    k_blk = k_ref[...]
    v_blk = v_ref[...]
    kt_blk = k_blk.astype(jnp.float32).T.astype(jnp.bfloat16)

    def tile(i, masked):
        start = pl.multiple_of(i * blk, blk)
        rows = pl.ds(start, blk)
        dk_new, dv_new = None, None
        qs = [q_ref[rows, g * head:(g + 1) * head] for g in range(per_kv)]
        dos = [do_ref[rows, g * head:(g + 1) * head] for g in range(per_kv)]
        scores = [dot(k_blk, qs[g], NT) for g in range(per_kv)]
        d_probs = [dot(v_blk, dos[g], NT) for g in range(per_kv)]
        if masked:
            scores = [causal_tile(s) for s in scores]
        for g in range(per_kv):
            p = jnp.exp2(scores[g] * c - lse_ref[0, g:g + 1, rows])
            ds = (p * (d_probs[g] - delta_ref[0, g:g + 1, rows])).astype(jnp.bfloat16)
            dv_g = dot(p.astype(jnp.bfloat16), dos[g])
            dk_g = dot(ds, qs[g])
            dk_new = dk_g if dk_new is None else dk_new + dk_g
            dv_new = dv_g if dv_new is None else dv_new + dv_g
            dqt_ref[g, :, rows] += dot(kt_blk, ds)
        return dk_new, dv_new

    dk_new, dv_new = tile(j, True)
    dk_acc[...] = dk_new
    dv_acc[...] = dv_new
    own = pl.ds(pl.multiple_of(j * blk, blk), blk)
    for g in range(per_kv):
        dq_ref[:, g * head:(g + 1) * head] = (dqt_ref[g, :, own] * scale).T.astype(jnp.bfloat16)

    def body(i, _):
        dk_new, dv_new = tile(i, False)
        dk_acc[...] += dk_new
        dv_acc[...] += dv_new
        return _

    lax.fori_loop(j + 1, blocks, body, 0)
    dk_ref[...] = (dk_acc[...] * scale).astype(jnp.bfloat16)
    dv_ref[...] = dv_acc[...].astype(jnp.bfloat16)


def attn_bwd(q, k, v, lse, delta, d_out, head):
    toks = q.shape[0]
    kv_heads = k.shape[1] // head
    per_kv = q.shape[1] // k.shape[1]
    wide = per_kv * head
    blocks = toks // BLOCK
    flops = 5 * 2 * toks * toks // 2 * q.shape[1]
    whole = pl.BlockSpec((toks, wide), lambda h, j: (0, h))
    stat = pl.BlockSpec((1, per_kv, toks), lambda h, j: (h, 0, 0))
    kv_spec = pl.BlockSpec((BLOCK, head), lambda h, j: (j, h))
    return pl.pallas_call(
        functools.partial(attn_bwd_kernel, head=head, per_kv=per_kv, blocks=blocks),
        grid=(kv_heads, blocks),
        in_specs=[whole, whole, stat, stat, kv_spec, kv_spec],
        out_specs=[pl.BlockSpec((BLOCK, wide), lambda h, j: (j, h)), kv_spec, kv_spec],
        out_shape=[jax.ShapeDtypeStruct(q.shape, jnp.bfloat16), jax.ShapeDtypeStruct(k.shape, jnp.bfloat16),
                   jax.ShapeDtypeStruct(v.shape, jnp.bfloat16)],
        scratch_shapes=[pltpu.VMEM((per_kv, head, toks), jnp.float32), pltpu.VMEM((BLOCK, head), jnp.float32),
                        pltpu.VMEM((BLOCK, head), jnp.float32)],
        compiler_params=pltpu.CompilerParams(dimension_semantics=('arbitrary', 'arbitrary'), vmem_limit_bytes=VMEM_LIMIT),
        cost_estimate=pl.CostEstimate(flops=2 * flops, bytes_accessed=(q.size + k.size) * 6, transcendentals=0),
        name='attn_bwd',
    )(q, d_out, lse, delta, k, v)


def solution(mesh):
    def to_seqs(arr):
        return lax.all_to_all(arr, 'sp', 0, 0, tiled=True).reshape(-1, arr.shape[2])

    def to_tokens(arr, shape):
        return lax.all_to_all(arr.reshape(shape), 'sp', 0, 0, tiled=True)

    def mm(lhs, rhs, dims):
        return lax.dot_general(lhs, rhs, (dims, ((), ())), preferred_element_type=jnp.float32)

    def reduce_grad(partial_sum):
        shard = lax.psum_scatter(partial_sum, 'sp', scatter_dimension=0, tiled=True)
        return lax.all_gather(shard.astype(jnp.bfloat16), 'sp', axis=0, tiled=True)

    def device_step(x_in, dy_in, positions, w_q, w_k, w_v, w_o, w_pre, w_post, q_norm, k_norm):
        width = x_in.shape[2]
        head = q_norm.shape[0]
        kv_heads = w_k.shape[1] // head
        w_pre = w_pre.reshape(1, width)
        w_post = w_post.reshape(1, width)
        x_seq = to_seqs(x_in)
        dy_seq = to_seqs(dy_in)
        pos_all = lax.all_gather(positions, 'sp', axis=0, tiled=True)
        cosines, sines = rope_tables(pos_all, head)
        toks = x_seq.shape[0]
        normed, = row_call(pre_norm_kernel, toks, [x_seq], [w_pre], [like(x_seq)], 0, x_seq.size * 100)
        q_proj = mm(normed, w_q, ((1,), (0,))).astype(jnp.bfloat16)
        k_proj = mm(normed, w_k, ((1,), (0,))).astype(jnp.bfloat16)
        v_proj = mm(normed, w_v, ((1,), (0,))).astype(jnp.bfloat16)
        q_rot, k_rot = norm_rope(q_proj, k_proj, cosines, sines, q_norm, k_norm, head)
        o_flat, lse = attn_fwd(q_rot, k_rot, v_proj, head)
        proj = mm(o_flat, w_o, ((1,), (0,))).astype(jnp.bfloat16)
        y_seq, d_proj, dw_post = row_call(post_norm_kernel, toks, [x_seq, proj, dy_seq], [w_post], [like(x_seq), like(x_seq)], width, x_seq.size * 300)
        y_out = to_tokens(y_seq, x_in.shape)
        dwo_part = mm(o_flat, d_proj, ((0,), (0,)))
        d_oflat = mm(d_proj, w_o, ((1,), (1,))).astype(jnp.bfloat16)
        dw_o = reduce_grad(dwo_part)
        delta = attn_delta(o_flat, d_oflat, kv_heads, head)
        dq_rot, dk_rot, dv_flat = attn_bwd(q_rot, k_rot, v_proj, lse, delta, d_oflat, head)
        dwv_part = mm(normed, dv_flat, ((0,), (0,)))
        dw_v = reduce_grad(dwv_part)
        dq_flat, dk_flat, dq_norm, dk_norm = norm_rope_bwd(dq_rot, dk_rot, q_proj, k_proj, cosines, sines, q_norm, k_norm, head)
        dwq_part = mm(normed, dq_flat, ((0,), (0,)))
        dw_q = reduce_grad(dwq_part)
        dwk_part = mm(normed, dk_flat, ((0,), (0,)))
        dw_k = reduce_grad(dwk_part)
        d_normed = (mm(dq_flat, w_q, ((1,), (1,))) + mm(dk_flat, w_k, ((1,), (1,)))
                    + mm(dv_flat, w_v, ((1,), (1,)))).astype(jnp.bfloat16)
        dx_seq, dw_pre = row_call(pre_norm_bwd_kernel, toks, [x_seq, d_normed, dy_seq], [w_pre], [like(x_seq)], width, x_seq.size * 200)
        dx_out = to_tokens(dx_seq, x_in.shape)
        small = (jnp.sum(dw_pre, axis=0), jnp.sum(dw_post, axis=0), dq_norm, dk_norm)
        dw_pre, dw_post, dq_norm, dk_norm = lax.psum(small, 'sp')
        return (y_out, dx_out, dw_q, dw_k, dw_v, dw_o, dw_pre, dw_post, dq_norm, dk_norm)

    token_spec = P('dp', 'sp', None)
    return jax.shard_map(device_step, mesh=mesh,
                         in_specs=(token_spec, token_spec, P(('dp', 'sp')), P(None, None), P(None, None), P(None, None), P(None, None), P(None), P(None), P(None), P(None)),
                         out_specs=(token_spec, token_spec, P('dp', None), P('dp', None), P('dp', None), P('dp', None), P('dp'), P('dp'), P('dp'), P('dp')),
                         check_vma=False)
```

time: 4100 us -> 2170 us (0.53)
  matrix products: 1340 us -> 493 us
  other arithmetic: 670 us -> 24.2 us
  Pallas kernels: 0 us -> 615 us
  blocking collectives: 1060 us -> 587 us
  local copies, waits for them, and re-layouts: 481 us -> 65.4 us
  waiting for transfers between devices: 477 us -> 328 us
    dot_general x36 -> x12, matrix products: 1340 us -> 493 us  [mm(): lax.dot_general(lhs, rhs, (dims, ((), ())), preferred_element_type=jnp.fl...]
    psum x1, blocking collectives: 1060 us -> 359 us  [device_step(): dw_pre, dw_post, dq_norm, dk_norm = lax.psum(small, 'sp')]
    pallas_call x0 -> x8, Pallas kernels: none -> 615 us  [the longest x1 247 us: attn_bwd(): pl.pallas_call(functools.partial(attn_bwd_kernel, head=head, per_kv=per_k...]
    all_to_all x8 -> x4, waiting for transfers between devices: 477 us -> 0.01 us  [the longest x2 0.01 us: to_seqs(): return lax.all_to_all(arr, 'sp', 0, 0, tiled=True).reshape(-1, arr.shape[2])]
    reduce_scatter x0 -> x4, waiting for transfers between devices: none -> 318 us  [reduce_grad(): shard = lax.psum_scatter(partial_sum, 'sp', scatter_dimension=0, tiled=True)]
    another operation x6 -> x0, other arithmetic: 280 us -> none
    all_gather x0 -> x1, blocking collectives: none -> 228 us  [device_step(): pos_all = lax.all_gather(positions, 'sp', axis=0, tiled=True)]
    reduce_sum x9 -> x4, other arithmetic: 196 us -> 0.09 us  [the longest x2 0.04 us: norm_rope_bwd(): return (dq_o, dk_o, jnp.sum(dqn, axis=0), jnp.sum(dkn, axis=0))]
  transfers between devices with their start and end apart: 8 -> 12, of which waited for: 4 -> 4; matrix products, arithmetic and copies ran while one was open for 29% -> 20% of each run, Pallas kernels for 0% -> 12%
where the time goes in v1:
time: 2170 us; the launch traced here: 2160 us
  Pallas kernels  615 us (28%)
  blocking collectives  587 us (27%)
  matrix products  493 us (23%)
  waiting for transfers between devices  328 us (15%)
  local copies, waits for them, and re-layouts  65.4 us (3%)
  starting transfers between devices  34.9 us (2%)
  other arithmetic  24.2 us (1%)
    dot_general x12, matrix products, mm(): lax.dot_general(lhs, rhs, (dims, ((), ())), preferred_element_type=jnp.fl...  493 us
    psum x1, blocking collectives, device_step(): dw_pre, dw_post, dq_norm, dk_norm = lax.psum(small, 'sp')  359 us
    reduce_scatter x4, waiting for transfers between devices, reduce_grad(): shard = lax.psum_scatter(partial_sum, 'sp', scatter_dimension=0, tiled=True)  318 us
    pallas_call x1, Pallas kernels, attn_bwd(): pl.pallas_call(functools.partial(attn_bwd_kernel, head=head, per_kv=per_k...  247 us
    all_gather x1, blocking collectives, device_step(): pos_all = lax.all_gather(positions, 'sp', axis=0, tiled=True)  228 us
    pallas_call x1, Pallas kernels, attn_fwd(): pl.pallas_call(functools.partial(attn_fwd_kernel, head=head, per_kv=per_k...  177 us
    pallas_call x3, Pallas kernels, row_call(): pl.pallas_call(body, grid=(toks // NORM_BLOCK,), in_specs=[rows(arr) for...  113 us
    unnamed x30, local copies, waits for them, and re-layouts  64.2 us
  transfers between devices with their start and end apart: 12, of which 4 were waited for; matrix products, arithmetic and copies ran while one was open for 20% of the time, Pallas kernels for 12%

profile of v1, /device:TPU:1, one launch (start us, length us, event | category | flops | bytes accessed | tf_op | source)
XLA Modules:
  0.0 2161.9 jit_solution(16176723489896090916)
XLA Ops:
  16.3 228.1 %all_gather.15 = s32[4096]{0:T(1024)S(1)} all-gather(s32[1024]{0:T(1024)S(1)} %copy-done.7), channel_id=1, replica_groups=mesh['dp'=2,'sp'=4] {'sp'}, dimensions={0}, use_global_device_ids=true | all-gather | bytes 20480 | tf_op jit(solution)/shard_map/all_gather | solution.py:386
  244.5 9.3 multiply_sine_fusion
  261.6 23.8 %shard_map.186 = bf16[4096,2560]{1,0:T(8,128)(2,1)} custom-call(bf16[4096,2560]{1,0:T(8,128)(2,1)} %bitcast.x_ref, f32[1,2560]{1,0:T(1,128)} %reshape.54.w_ref), custom_call_target="tpu_custom_call" | custom-call | flops 1048576000 | bytes 41943040 | tf_op jit(solution)/shard_map/pallas_call | solution.py:36
  285.4 27.8 %convolution_convert_fusion.3.v_ref = bf16[4096,1024]{1,0:T(8,128)(2,1)} fusion(bf16[4096,2560]{1,0:T(8,128)(2,1)} %shard_map.186, bf16[2560,1024]{1,0:T(8,128)(2,1)} %param.16), kind=kOutput, calls=%fused_computation.4 | convolution fusion | flops 21479030784 | bytes 34603008 | tf_op jit(solution)/shard_map/dot_general | solution.py:372
  313.3 23.6 %convolution_convert_fusion.4.k_ref = bf16[4096,1024]{1,0:T(8,128)(2,1)} fusion(bf16[4096,2560]{1,0:T(8,128)(2,1)S(1)} %copy-done, bf16[2560,1024]{1,0:T(8,128)(2,1)S(1)} %bitcast.37), kind=kOutput, calls=%fused_computation.5 | convolution fusion | flops 21479030784 | bytes 34603008 | tf_op jit(solution)/shard_map/dot_general | solution.py:372
  336.9 50.0 %convolution_convert_fusion.2.q_ref = bf16[4096,2048]{1,0:T(8,128)(2,1)} fusion(bf16[4096,2560]{1,0:T(8,128)(2,1)S(1)} %copy-done, bf16[2560,2048]{1,0:T(8,128)(2,1)} %param.14), kind=kOutput, calls=%fused_computation.3 | convolution fusion | flops 42958061568 | bytes 48234496 | tf_op jit(solution)/shard_map/dot_general | solution.py:372
  386.9 24.6 %norm_rope.1 = (bf16[4096,2048]{1,0:T(8,128)(2,1)}, bf16[4096,1024]{1,0:T(8,128)(2,1)}) custom-call(bf16[4096,2048]{1,0:T(8,128)(2,1)} %convolution_convert_fusion.2.q_ref, bf16[4096,1024]{1,0:T(8,128)(2,1)} %convolution_convert_fusion.4.k_ref, f32[4096,128]{1,0:T(8,128)} %get-tuple-element.47.cos_ref, f32[4096,128]{1,0:T(8,128)} %get-tuple-element.46.sin_ref, ...), custom_call_target="tpu_custom_call" | custom-call | flops 2516582400 | bytes 50331648 | tf_op jit(solution)/shard_map/norm_rope/pallas_call | solution.py:119
  411.5 177.1 %attn_fwd.1 = (bf16[4096,2048]{1,0:T(8,128)(2,1)}, f32[4,2,4096]{2,1,0:T(2,128)}) custom-call(bf16[4096,2048]{1,0:T(8,128)(2,1)} %get-tuple-element.26.q_ref, bf16[4096,1024]{1,0:T(8,128)(2,1)} %get-tuple-element.27.k_ref, bf16[4096,1024]{1,0:T(8,128)(2,1)} %convolution_convert_fusion.3.v_ref), custom_call_target="tpu_custom_call" | custom-call | flops 137438953472 | bytes 50331648 | tf_op jit(solution)/shard_map/attn_fwd/pallas_call | solution.py:246
  588.6 50.8 %convolution_convert_fusion.proj_ref = bf16[4096,2560]{1,0:T(8,128)(2,1)} fusion(bf16[4096,2048]{1,0:T(8,128)(2,1)} %get-tuple-element.28.o_ref, bf16[2048,2560]{1,0:T(8,128)(2,1)} %param.17), kind=kOutput, calls=%fused_computation.1 | convolution fusion | flops 42960158720 | bytes 48234496 | tf_op jit(solution)/shard_map/dot_general | solution.py:372
  639.4 47.2 %shard_map.187 = (bf16[4096,2560]{1,0:T(8,128)(2,1)}, bf16[4096,2560]{1,0:T(8,128)(2,1)}, f32[8,2560]{1,0:T(8,128)}) custom-call(bf16[4096,2560]{1,0:T(8,128)(2,1)} %bitcast.x_ref, bf16[4096,2560]{1,0:T(8,128)(2,1)} %convolution_convert_fusion.proj_ref, bf16[4096,2560]{1,0:T(8,128)(2,1)} %bitcast.3.dy_ref, f32[1,2560]{1,0:T(1,128)} %reshape.58.w_ref), custom_call_target="tpu_custom_call" | custom-call | flops 3145728000 | bytes 104857600 | tf_op jit(solution)/shard_map/pallas_call | solution.py:36
  686.6 51.0 %convolution_convert_fusion.1.do_ref = bf16[4096,2048]{1,0:T(8,128)(2,1)} fusion(bf16[4096,2560]{1,0:T(8,128)(2,1)} %get-tuple-element.30, bf16[2048,2560]{1,0:T(8,128)(2,1)} %param.17), kind=kOutput, calls=%fused_computation.2 | convolution fusion | flops 42958061568 | bytes 48234496 | tf_op jit(solution)/shard_map/dot_general | solution.py:372
  737.6 17.6 attn_delta.1.delta_ref
  755.2 247.1 %attn_bwd.1 = (bf16[4096,2048]{1,0:T(8,128)(2,1)}, bf16[4096,1024]{1,0:T(8,128)(2,1)}, bf16[4096,1024]{1,0:T(8,128)(2,1)}) custom-call(bf16[4096,2048]{1,0:T(8,128)(2,1)} %get-tuple-element.26.q_ref, bf16[4096,2048]{1,0:T(8,128)(2,1)} %convolution_convert_fusion.1.do_ref, f32[4,2,4096]{2,1,0:T(2,128)} %get-tuple-element.31.lse_ref, ...), custom_call_target="tpu_custom_call" | custom-call | flops 343597383680 | bytes 75497472 | tf_op jit(solution)/shard_map/attn_bwd/pallas_call | solution.py:349
  1002.3 34.9 %norm_rope_bwd.1 = (bf16[4096,2048]{1,0:T(8,128)(2,1)}, bf16[4096,1024]{1,0:T(8,128)(2,1)}, f32[8,256]{1,0:T(8,128)}, f32[8,256]{1,0:T(8,128)}) custom-call(bf16[4096,2048]{1,0:T(8,128)(2,1)} %get-tuple-element.32.dq_ref, bf16[4096,1024]{1,0:T(8,128)(2,1)} %get-tuple-element.33.dk_ref, bf16[4096,2048]{1,0:T(8,128)(2,1)} %convolution_convert_fusion.2.q_ref, ...), custom_call_target="tpu_custom_call" | custom-call | flops 3774873600 | bytes 75497472 | tf_op jit(solution)/shard_map/norm_rope_bwd/pallas_call | solution.py:173
  1037.2 29.0 %fusion.3 = f32[2560,1024]{1,0:T(8,128)} fusion(bf16[4096,2560]{1,0:T(8,128)(2,1)} %shard_map.186, bf16[4096,1024]{1,0:T(8,128)(2,1)} %get-tuple-element.35), kind=kOutput, calls=%fused_computation.13 | convolution fusion | flops 21474836480 | bytes 39845888 | tf_op jit(solution)/shard_map/dot_general | solution.py:372
  1066.3 29.1 %fusion.4 = f32[2560,1024]{1,0:T(8,128)} fusion(bf16[4096,2560]{1,0:T(8,128)(2,1)} %shard_map.186, bf16[4096,1024]{1,0:T(8,128)(2,1)} %get-tuple-element.36), kind=kOutput, calls=%fused_computation.14 | convolution fusion | flops 21474836480 | bytes 39845888 | tf_op jit(solution)/shard_map/dot_general | solution.py:372
  1095.4 55.1 %fusion.5 = f32[2048,2560]{1,0:T(8,128)} fusion(bf16[4096,2048]{1,0:T(8,128)(2,1)} %get-tuple-element.28.o_ref, bf16[4096,2560]{1,0:T(8,128)(2,1)} %get-tuple-element.30), kind=kOutput, calls=%fused_computation.15 | convolution fusion | flops 42949672960 | bytes 58720256 | tf_op jit(solution)/shard_map/dot_general | solution.py:372
  1150.6 56.2 %fusion.2 = f32[2560,2048]{1,0:T(8,128)} fusion(bf16[4096,2560]{1,0:T(8,128)(2,1)} %shard_map.186, bf16[4096,2048]{1,0:T(8,128)(2,1)} %get-tuple-element.34), kind=kOutput, calls=%fused_computation.12 | convolution fusion | flops 42949672960 | bytes 58720256 | tf_op jit(solution)/shard_map/dot_general | solution.py:372
  1210.0 18.9 reduce-scatter.9.cloned.1.call-done
  1231.9 10.5 all-to-all-start.2
  1242.4 252.1 %reduce-scatter.11.cloned.1.call-done = f32[512,2560]{1,0:T(8,128)} async-done(((f32[2048,2560]{1,0:T(8,128)}), f32[512,2560]{1,0:T(8,128)}) %reduce-scatter.11.cloned.1.call-update) | async-done | bytes 5242896 | tf_op jit(solution)/shard_map/reduce_scatter | solution.py:375
  1498.9 32.1 %fusion.1 = f32[4096,2560]{1,0:T(8,128)} fusion(bf16[4096,1024]{1,0:T(8,128)(2,1)} %get-tuple-element.36, bf16[2560,1024]{1,0:T(8,128)(2,1)} %param.16), kind=kOutput, calls=%fused_computation.11 | convolution fusion | flops 21474836480 | bytes 55574528 | tf_op jit(solution)/shard_map/dot_general | solution.py:372
  1531.0 28.0 %fusion = f32[4096,2560]{1,0:T(8,128)} fusion(bf16[4096,1024]{1,0:T(8,128)(2,1)} %get-tuple-element.35, bf16[2560,1024]{1,0:T(8,128)(2,1)S(1)} %bitcast.39), kind=kOutput, calls=%fused_computation.10 | convolution fusion | flops 21474836480 | bytes 55574528 | tf_op jit(solution)/shard_map/dot_general | solution.py:372
  1559.1 60.3 %add_convert_fusion.dn_ref = bf16[4096,2560]{1,0:T(8,128)(2,1)} fusion(f32[4096,2560]{1,0:T(8,128)} %fusion.1, f32[4096,2560]{1,0:T(8,128)} %fusion, bf16[4096,2048]{1,0:T(8,128)(2,1)} %get-tuple-element.34, bf16[2560,2048]{1,0:T(8,128)(2,1)} %param.14), kind=kOutput, calls=%fused_computation | convolution fusion | flops 42981130240 | bytes 132120576 | tf_op jit(solution)/shard_map/dot_general | solution.py:372
  1619.4 42.4 %shard_map.188 = (bf16[4096,2560]{1,0:T(8,128)(2,1)}, f32[8,2560]{1,0:T(8,128)}) custom-call(bf16[4096,2560]{1,0:T(8,128)(2,1)} %bitcast.x_ref, bf16[4096,2560]{1,0:T(8,128)(2,1)} %add_convert_fusion.dn_ref, bf16[4096,2560]{1,0:T(8,128)(2,1)} %bitcast.3.dy_ref, f32[1,2560]{1,0:T(1,128)} %reshape.54.w_ref), custom_call_target="tpu_custom_call" | custom-call | flops 2097152000 | bytes 83886080 | tf_op jit(solution)/shard_map/pallas_call | solution.py:36
  1670.2 47.2 %reduce-scatter.5.cloned.1.call-done = f32[640,2048]{1,0:T(8,128)} async-done(((f32[2560,2048]{1,0:T(8,128)}), f32[640,2048]{1,0:T(8,128)}) %reduce-scatter.5.cloned.1.call-update) | async-done | bytes 5242896 | tf_op jit(solution)/shard_map/reduce_scatter | solution.py:375
  1722.0 358.5 %all-reduce = (f32[2560]{0:T(1024)}, f32[2560]{0:T(1024)}, f32[256]{0:T(256)}, f32[256]{0:T(256)}) all-reduce(f32[2560]{0:T(1024)S(1)} %reduce_sum.36, f32[2560]{0:T(1024)S(1)} %reduce_sum.37, f32[256]{0:T(256)S(1)} %reduce_sum.38, f32[256]{0:T(256)S(1)} %reduce_sum.39), channel_id=1, replica_groups=mesh['dp'=2,'sp'=4] {'sp'}, use_global_device_ids=true, to_apply=%region_5.0 | all-reduce | flops 5632 | bytes 45056 | tf_op jit(solution)/shard_map/psum | solution.py:415
  2080.5 9.9 all-gather.5.cloned.1.call-done
  2090.4 17.1 copy.27
  2107.6 17.1 copy.28
  2124.7 10.3 copy.29
  2145.8 8.7 copy.32
  (67 shorter events, 51.6 us)
Async XLA Ops:
  7.2 7.9 copy-start.3
  7.2 8.5 copy-start.4
  7.2 9.1 copy-start.7
  7.2 246.5 %all-to-all-start = ((bf16[4,1024,2560]{2,1,0:T(8,128)(2,1)}), bf16[4,1024,2560]{2,1,0:T(8,128)(2,1)}, u32[]{:S(2)}, u32[]{:S(2)}) async-start(bf16[4,1024,2560]{2,1,0:T(8,128)(2,1)} %param.11), calls=%async_computation | async-start | bytes 41943040 | tf_op jit(solution)/shard_map/all_to_all | solution.py:366
  253.7 385.6 %all-to-all-start.1 = ((bf16[4,1024,2560]{2,1,0:T(8,128)(2,1)}), bf16[4,1024,2560]{2,1,0:T(8,128)(2,1)}, u32[]{:S(2)}, u32[]{:S(2)}) async-start(bf16[4,1024,2560]{2,1,0:T(8,128)(2,1)} %param.12), calls=%async_computation.1 | async-start | bytes 41943040 | tf_op jit(solution)/shard_map/all_to_all | solution.py:366
  261.6 945.2 %reduce-scatter.7.cloned.1.call-start = ((), (), s32[]{:S(2)}) async-start(), calls=%async_computation.10 | async-start | bytes 13107200 | tf_op jit(solution)/shard_map/reduce_scatter | solution.py:375
  261.6 51.6 %slice-start = ((s8[5242880]{0:T(1024)(128)(4,1)}), s8[1048576]{0:T(1024)(128)(4,1)S(1)}, s32[]{:S(2)}) async-start(s8[5242880]{0:T(1024)(128)(4,1)} %bitcast.36), calls=%async_computation.16 | async-start | bytes 2097152
  285.4 27.8 %copy-start = (bf16[4096,2560]{1,0:T(8,128)(2,1)S(1)}, bf16[4096,2560]{1,0:T(8,128)(2,1)}, u32[]{:S(2)}) copy-start(bf16[4096,2560]{1,0:T(8,128)(2,1)} %shard_map.186) | copy-start | bytes 62914564
  285.4 27.8 %slice-start.1 = ((s8[5242880]{0:T(1024)(128)(4,1)}), s8[4194304]{0:T(1024)(128)(4,1)S(1)}, s32[]{:S(2)}) async-start(s8[5242880]{0:T(1024)(128)(4,1)} %bitcast.36), calls=%async_computation.17 | async-start | bytes 8388608
  1066.2 162.7 %reduce-scatter.9.cloned.1.call-start = ((), (), s32[]{:S(2)}) async-start(), calls=%async_computation.12 | async-start | bytes 13107200 | tf_op jit(solution)/shard_map/reduce_scatter | solution.py:375
  1095.3 399.2 %reduce-scatter.11.cloned.1.call-start = ((), (), s32[]{:S(2)}) async-start(), calls=%async_computation.14 | async-start | bytes 26214400 | tf_op jit(solution)/shard_map/reduce_scatter | solution.py:375
  1150.5 566.9 %reduce-scatter.5.cloned.1.call-start = ((), (), s32[]{:S(2)}) async-start(), calls=%async_computation.8 | async-start | bytes 26214400 | tf_op jit(solution)/shard_map/reduce_scatter | solution.py:375
  1206.8 873.7 %all-gather.7.cloned.1.call-start = ((), (), s32[]{:S(2)}) async-start(), calls=%async_computation.11 | async-start | bytes 6553600 | tf_op jit(solution)/shard_map/all_gather | solution.py:376
  1210.0 870.5 %all-gather.9.cloned.1.call-start = ((), (), s32[]{:S(2)}) async-start(), calls=%async_computation.13 | async-start | bytes 6553600 | tf_op jit(solution)/shard_map/all_gather | solution.py:376
  1231.9 429.8 %all-to-all-start.2 = ((bf16[4,1024,2560]{2,1,0:T(8,128)(2,1)}), bf16[4,1024,2560]{2,1,0:T(8,128)(2,1)}, u32[]{:S(2)}, u32[]{:S(2)}) async-start(bf16[4,1024,2560]{2,1,0:T(8,128)(2,1)} %bitcast.30), calls=%async_computation.2 | async-start | bytes 41943040 | tf_op jit(solution)/shard_map/all_to_all | solution.py:369
  1242.4 838.1 %all-gather.11.cloned.1.call-start = ((), (), s32[]{:S(2)}) async-start(), calls=%async_computation.15 | async-start | bytes 13107200 | tf_op jit(solution)/shard_map/all_gather | solution.py:376
  1494.5 36.5 %slice-start.2 = ((s8[5242880]{0:T(1024)(128)(4,1)}), s8[1048576]{0:T(1024)(128)(4,1)S(1)}, s32[]{:S(2)}) async-start(s8[5242880]{0:T(1024)(128)(4,1)} %bitcast.38), calls=%async_computation.18 | async-start | bytes 2097152
  1498.9 32.1 %slice-start.3 = ((s8[5242880]{0:T(1024)(128)(4,1)}), s8[4194304]{0:T(1024)(128)(4,1)S(1)}, s32[]{:S(2)}) async-start(s8[5242880]{0:T(1024)(128)(4,1)} %bitcast.38), calls=%async_computation.19 | async-start | bytes 8388608
  1661.7 60.1 %copy-start.1 = (f32[8,2560]{1,0:T(8,128)S(1)}, f32[8,2560]{1,0:T(8,128)}, u32[]{:S(2)}) copy-start(f32[8,2560]{1,0:T(8,128)} %get-tuple-element.39) | copy-start | bytes 245764
  1661.8 60.1 %copy-start.6 = (f32[8,256]{1,0:T(8,128)S(1)}, f32[8,256]{1,0:T(8,128)}, u32[]{:S(2)}) copy-start(f32[8,256]{1,0:T(8,128)} %get-tuple-element.40) | copy-start | bytes 24580
  1661.8 60.2 %copy-start.5 = (f32[8,256]{1,0:T(8,128)S(1)}, f32[8,256]{1,0:T(8,128)}, u32[]{:S(2)}) copy-start(f32[8,256]{1,0:T(8,128)} %get-tuple-element.41) | copy-start | bytes 24580
  1661.8 60.2 %copy-start.2 = (f32[8,2560]{1,0:T(8,128)S(1)}, f32[8,2560]{1,0:T(8,128)}, u32[]{:S(2)}) copy-start(f32[8,2560]{1,0:T(8,128)} %get-tuple-element.38) | copy-start | bytes 245764
  1661.8 418.7 %all-to-all-start.3 = ((bf16[4,1024,2560]{2,1,0:T(8,128)(2,1)}), bf16[4,1024,2560]{2,1,0:T(8,128)(2,1)}, u32[]{:S(2)}, u32[]{:S(2)}) async-start(bf16[4,1024,2560]{2,1,0:T(8,128)(2,1)} %bitcast.31), calls=%async_computation.3 | async-start | bytes 41943040 | tf_op jit(solution)/shard_map/all_to_all | solution.py:369
  1670.2 420.2 %all-gather.5.cloned.1.call-start = ((), (), s32[]{:S(2)}) async-start(), calls=%async_computation.9 | async-start | bytes 13107200 | tf_op jit(solution)/shard_map/all_gather | solution.py:376
Sparse Core Ops, SparseCore 0:
  1066.3 80.4 reduce-scatter.6
  1150.0 78.8 reduce-scatter.8
  1232.0 262.4 reduce-scatter.10
  1496.9 220.4 reduce-scatter.4
  1719.4 66.4 all-gather.6
  1787.9 65.7 all-gather.8
  1855.8 123.6 all-gather.10
  1981.6 108.7 all-gather.4
